TPU v7x, 32 devices: a whole 2x2x4 slice. The times are simulated.
32 devices in a mesh: dp: 4 (over y, x), shard: 8 (over z, core).
Axes of the slice: x: 2, y: 2, z: 4, core: 2. Of those that a mesh axis runs over, the one named last changes fastest.
Arguments:
- gradients: bfloat16 [4, 1536, 2048], P('dp', 'shard'), may hold values from -4000 to 4000, as said below
- master_weights: float32 [1536, 2048], P(('shard', 'dp')), may hold values from -6 to 6
- first_moment: float32 [1536, 2048], P(('shard', 'dp')), may hold values from -4 to 4
- second_moment: float32 [1536, 2048], P(('shard', 'dp')), may hold values from 0.05 to 2
Outputs:
- parameters: bfloat16 [1536, 2048], P('shard')
- new_master: float32 [1536, 2048], P(('shard', 'dp'))
- new_first: float32 [1536, 2048], P(('shard', 'dp'))
- new_second: float32 [1536, 2048], P(('shard', 'dp'))
Inputs may be any that keep to these rules, and one draw needn't show every extreme that they name: `gradients`: each replica's partial gradient.
All inputs are finite; a program needn't handle non-finite values.
Results may differ from a plain program's by a relative error of at most 0.006.
Values may be sent and summed in bfloat16 or wider, within the bound.
A program may use at most 64 MiB of HBM per device.

v0:
```python
import math

import jax
import jax.numpy as jnp
from jax import lax
from jax.sharding import PartitionSpec as P

first_bias = 1.0 - math.exp(100.0 * math.log(0.9))
second_bias = 1.0 - math.exp(100.0 * math.log(0.95))


def adam_update(summed, factor, master_weights, first_moment, second_moment):
    clipped = factor * summed
    new_first = 0.9 * first_moment + 0.1 * clipped
    new_second = 0.95 * second_moment + 0.05 * clipped * clipped
    first_hat = new_first / first_bias
    second_hat = new_second / second_bias
    new_master = master_weights - 0.01 * (
        first_hat / (jnp.sqrt(second_hat) + 1e-08) + 0.1 * master_weights
    )
    return (new_master, new_first, new_second)


def per_device(gradients, master_weights, first_moment, second_moment):
    rows_dev = master_weights.shape[0]
    width = master_weights.shape[1]
    entries = rows_dev * lax.axis_size("dp") * lax.axis_size("shard") * width
    local_grad = gradients[0].astype(jnp.float32)
    group_sum = lax.psum(local_grad.astype(jnp.bfloat16), "dp").astype(jnp.float32)
    square_sum = lax.psum(jnp.sum(group_sum * group_sum), "shard")
    summed = lax.dynamic_slice_in_dim(group_sum, lax.axis_index("dp") * rows_dev, rows_dev, 0)
    limit = 0.5 * math.sqrt(entries)
    factor = jnp.minimum(1.0, limit / jnp.sqrt(square_sum + 1e-06))
    new_master, new_first, new_second = adam_update(
        summed, factor, master_weights, first_moment, second_moment
    )
    owned_params = new_master.astype(jnp.bfloat16)
    parameters = lax.all_gather(owned_params, "dp", axis=0, tiled=True)
    return (parameters, new_master, new_first, new_second)


def solution(mesh):
    in_specs = (
        P("dp", "shard", None),
        P(("shard", "dp"), None),
        P(("shard", "dp"), None),
        P(("shard", "dp"), None),
    )
    out_specs = (
        P("shard", None),
        P(("shard", "dp"), None),
        P(("shard", "dp"), None),
        P(("shard", "dp"), None),
    )
    return jax.shard_map(
        per_device, mesh=mesh, in_specs=in_specs, out_specs=out_specs, check_vma=False
    )
```

profile of v0, /device:TPU:0, one launch (start us, length us, event | category | flops | bytes accessed | tf_op | source)
XLA Modules:
  0.0 104.0 jit_solution(5582572716141292494)
XLA Ops:
  7.2 0.0 all-reduce.2.cloned.1.call-start
  7.2 0.7 all-reduce.2.cloned.1.call-update
  7.9 0.0 copy-start
  7.9 0.0 copy-start.1
  7.9 0.0 copy-start.2
  7.9 54.5 %all-reduce.2.cloned.1.call-done = bf16[192,2048]{1,0:T(8,128)(2,1)} async-done(((bf16[192,2048]{1,0:T(8,128)(2,1)}), bf16[192,2048]{1,0:T(8,128)(2,1)}) %all-reduce.2.cloned.1.call-update) | async-done | bytes 786448 | tf_op jit(solution)/shard_map/psum | solution.py:29
  62.4 2.1 %multiply_reduce_fusion = f32[]{:T(128)} fusion(bf16[192,2048]{1,0:T(8,128)(2,1)} %all-reduce.2.cloned.1.call-done), kind=kLoop, calls=%fused_computation | loop fusion | flops 1179647 | bytes 786436 | tf_op jit(solution)/shard_map/reduce_sum | solution.py:30
  64.6 16.9 %psum.15 = f32[]{:T(128)} all-reduce(f32[]{:T(128)} %multiply_reduce_fusion), channel_id=1, replica_groups=mesh['dp'=4,'shard'=8] {'shard'}, use_global_device_ids=true, to_apply=%region_2.0 | all-reduce | flops 1 | bytes 8 | tf_op jit(solution)/shard_map/psum | solution.py:30
  82.1 1.3 %convert_element_type.8 = f32[192,2048]{1,0:T(8,128)S(1)} convert(bf16[192,2048]{1,0:T(8,128)(2,1)} %all-reduce.2.cloned.1.call-done) | non-fusion elementwise | flops 393216 | bytes 2359296 | tf_op jit(solution)/shard_map/convert_element_type | solution.py:29
  83.4 0.0 copy-done
  83.4 0.0 copy-done.1
  83.4 0.0 copy-done.2
  83.4 1.2 %fusion.1 = (bf16[48,2048]{1,0:T(8,128)(2,1)S(1)}, f32[48,2048]{1,0:T(8,128)}, f32[48,2048]{1,0:T(8,128)}, f32[48,2048]{1,0:T(8,128)}) fusion(f32[48,2048]{1,0:T(8,128)S(1)} %copy-done, f32[192,2048]{1,0:T(8,128)S(1)} %convert_element_type.8, s32[]{:T(128)S(6)} %select_n.3, f32[]{:T(128)S(6)} %min_shard_map.3, f32[48,2048]{1,0:T(8,128)S(1)} %copy-done.1, ...), kind=kLoop, calls=%fused_computation.6 | loop fusion | flops 1671168 | bytes 2949128 | tf_op jit(solution)/shard_map/convert_element_type | solution.py:37
  84.6 11.7 %all_gather.3 = bf16[192,2048]{1,0:T(8,128)(2,1)S(1)} all-gather(bf16[48,2048]{1,0:T(8,128)(2,1)S(1)} %get-tuple-element.4), channel_id=1, replica_groups=mesh['dp'=4,'shard'=8] {'dp'}, dimensions={0}, use_global_device_ids=true | all-gather | bytes 983040 | tf_op jit(solution)/shard_map/all_gather | solution.py:38
  96.3 0.9 copy.11
Async XLA Ops:
  7.2 55.2 %all-reduce.2.cloned.1.call-start = ((), (), s32[]{:S(2)}) async-start(), calls=%async_computation | async-start | bytes 1572864 | tf_op jit(solution)/shard_map/psum | solution.py:29
  7.9 75.5 %copy-start = (f32[48,2048]{1,0:T(8,128)S(1)}, f32[48,2048]{1,0:T(8,128)}, u32[]{:S(2)}) copy-start(f32[48,2048]{1,0:T(8,128)} %param.5) | copy-start | bytes 1179652
  7.9 75.5 %copy-start.1 = (f32[48,2048]{1,0:T(8,128)S(1)}, f32[48,2048]{1,0:T(8,128)}, u32[]{:S(2)}) copy-start(f32[48,2048]{1,0:T(8,128)} %param.6) | copy-start | bytes 1179652
  7.9 75.5 %copy-start.2 = (f32[48,2048]{1,0:T(8,128)S(1)}, f32[48,2048]{1,0:T(8,128)}, u32[]{:S(2)}) copy-start(f32[48,2048]{1,0:T(8,128)} %param.7) | copy-start | bytes 1179652
Sparse Core Ops, SparseCore 0:
  11.0 51.3 all-reduce.1
where the time goes:
time: 104 us
  waiting for transfers between devices  55.2 us (53%)
  blocking collectives  28.5 us (27%)
  between operations  14.8 us (14%)
  other arithmetic  4.65 us (4%)
    psum x1, waiting for transfers between devices, per_device(): lax.psum(local_grad.astype(jnp.bfloat16), 'dp').astype(jnp.float32)  54.5 us
    psum x1, blocking collectives, per_device(): square_sum = lax.psum(jnp.sum(group_sum * group_sum), 'shard')  16.9 us
    all_gather x1, blocking collectives, per_device(): parameters = lax.all_gather(owned_params, 'dp', axis=0, tiled=True)  11.7 us
    reduce_sum x1, other arithmetic, per_device(): square_sum = lax.psum(jnp.sum(group_sum * group_sum), 'shard')  2.14 us
  transfers between devices with their start and end apart: 1, of which 1 were waited for; matrix products, arithmetic and copies ran while one was open for 0% of the time, Pallas kernels for 0%

commit v1 on v0

v1 whole, which is shorter than its diff:
```python
import functools
import math

import jax
import jax.numpy as jnp
from jax import lax
from jax.experimental import pallas as pl
from jax.experimental.pallas import tpu as pltpu
from jax.sharding import PartitionSpec as P

MESH = pl.DeviceIdType.MESH
first_bias = 1.0 - math.exp(100.0 * math.log(0.9))
second_bias = 1.0 - math.exp(100.0 * math.log(0.95))


def grid_of(n_dp):
    ny = max(d for d in range(1, math.isqrt(n_dp) + 1) if n_dp % d == 0)
    return ny, n_dp // ny


def copies_of(ny, nx, n_sh):
    return 4 * ny * nx + 2 * (ny + nx) + ny * nx + n_sh


def step_kernel(
    ny, nx, n_sh, entries,
    g, w, m, v,
    out_p, out_w, out_m, out_v,
    gv, wv, mv, vv, sv, pv,
    r1a, r1b, s2a, s2b, r2a, r2b, fa, fb,
    d_own, d_in, h_own, h_in,
    lsem, ssem, rsem,
):
    n_dp = ny * nx
    rows, width = w.shape
    half = width // 2
    tile_r = 16 if rows % 16 == 0 else rows
    tile_c = 512 if half % 512 == 0 else half
    me = lax.axis_index("dp")
    sh = lax.axis_index("shard")
    y, x = me // nx, lax.rem(me, nx)
    count = [0]
    local_count = [0]
    started = []
    local_started = []

    def at_y(k):
        return lax.rem(y + k, ny)

    def at_x(j):
        return lax.rem(x + j, nx)

    def block(by, bx):
        return pl.ds(pl.multiple_of((by * nx + bx) * rows, rows), rows)

    def send(src, dst, target):
        i = count[0]
        count[0] += 1
        copy = pltpu.make_async_remote_copy(
            src_ref=src, dst_ref=dst, send_sem=ssem.at[i], recv_sem=rsem.at[i],
            device_id=target, device_id_type=MESH,
        )
        copy.start()
        started.append(copy)
        return copy

    def local(src, dst):
        i = local_count[0]
        local_count[0] += 1
        copy = pltpu.make_async_copy(src, dst, lsem.at[i])
        copy.start()
        return copy

    barrier = pltpu.get_barrier_semaphore()
    for i in range(1, n_dp):
        pl.semaphore_signal(
            barrier, inc=1, device_id={"dp": lax.rem(me + i, n_dp)}, device_id_type=MESH
        )
    for i in range(1, n_sh):
        pl.semaphore_signal(
            barrier, inc=1, device_id={"shard": lax.rem(sh + i, n_sh)}, device_id_type=MESH
        )
    grads_in = local(g.at[0], gv)
    state_in = [local(w, wv), local(m, mv), local(v, vv)]
    grads_in.wait()
    pl.semaphore_wait(barrier, n_dp - 1 + n_sh - 1)

    cols_a, cols_b = pl.ds(0, half), pl.ds(half, half)

    first_a, first_b = {}, {}
    for j in list(range(1, nx)) + [0]:
        for k in range(1, ny):
            first_a[k, j] = send(
                gv.at[block(at_y(k), at_x(j)), cols_a], r1a.at[k - 1, j],
                {"dp": at_y(k) * nx + x},
            )
    for k in list(range(1, ny)) + [0]:
        for j in range(1, nx):
            first_b[j, k] = send(
                gv.at[block(at_y(k), at_x(j)), cols_b], r1b.at[j - 1, k],
                {"dp": y * nx + at_x(j)},
            )

    def tiles():
        for r in range(0, rows, tile_r):
            for c in range(0, half, tile_c):
                yield r, c

    def own_rows(by, bx, r):
        start = pl.multiple_of((by * nx + bx) * rows + r, tile_r)
        return pl.ds(start, tile_r)

    second_a, second_b = [], []
    for j in range(1, nx):
        for k in range(1, ny):
            first_a[k, j].wait_recv()
        for r, c in tiles():
            here = (pl.ds(r, tile_r), pl.ds(c, tile_c))
            part = gv[own_rows(y, at_x(j), r), pl.ds(c, tile_c)].astype(jnp.float32)
            for k in range(1, ny):
                part = part + r1a[(k - 1, j) + here].astype(jnp.float32)
            s2a[(j - 1,) + here] = part.astype(jnp.bfloat16)
        second_a.append(send(s2a.at[j - 1], r2a.at[j - 1], {"dp": y * nx + at_x(j)}))
    for k in range(1, ny):
        for j in range(1, nx):
            first_b[j, k].wait_recv()
        for r, c in tiles():
            here = (pl.ds(r, tile_r), pl.ds(c, tile_c))
            part = gv[own_rows(at_y(k), x, r), pl.ds(half + c, tile_c)].astype(jnp.float32)
            for j in range(1, nx):
                part = part + r1b[(j - 1, k) + here].astype(jnp.float32)
            s2b[(k - 1,) + here] = part.astype(jnp.bfloat16)
        second_b.append(send(s2b.at[k - 1], r2b.at[k - 1], {"dp": at_y(k) * nx + x}))

    for k in range(1, ny):
        first_a[k, 0].wait_recv()
    for j in range(1, nx):
        first_b[j, 0].wait_recv()
    squares = jnp.zeros((8, 128), jnp.float32)
    for base, first, first_n, second, later in (
        (0, r1a, ny - 1, r2a, second_a), (half, r1b, nx - 1, r2b, second_b)
    ):
        for copy in later:
            copy.wait_recv()
        for r, c in tiles():
            here = (pl.ds(r, tile_r), pl.ds(c, tile_c))
            total = gv[own_rows(y, x, r), pl.ds(base + c, tile_c)].astype(jnp.float32)
            for i in range(first_n):
                total = total + first[(i, 0) + here].astype(jnp.float32)
            for i in range(len(later)):
                total = total + second[(i,) + here].astype(jnp.float32)
            sv[pl.ds(r, tile_r), pl.ds(base + c, tile_c)] = total
            square = total * total
            for a in range(0, tile_r, 8):
                for b in range(0, tile_c, 128):
                    squares = squares + square[a:a + 8, b:b + 128]

    d_own[...] = squares
    over_dp = [
        send(d_own, d_in.at[i - 1], {"dp": lax.rem(me + i, n_dp)}) for i in range(1, n_dp)
    ]
    for i, copy in enumerate(over_dp):
        copy.wait_recv()
        squares = squares + d_in[i]
    h_own[...] = squares
    over_sh = [
        send(h_own, h_in.at[i - 1], {"shard": lax.rem(sh + i, n_sh)}) for i in range(1, n_sh)
    ]
    for copy in state_in:
        copy.wait()
    for i, copy in enumerate(over_sh):
        copy.wait_recv()
        squares = squares + h_in[i]
    square_sum = jnp.sum(jnp.sum(squares, axis=0, keepdims=True), axis=1, keepdims=True)
    limit = 0.5 * math.sqrt(entries)
    factor = jnp.minimum(1.0, limit / jnp.sqrt(square_sum + 1e-06))

    def update(base):
        for r, c in tiles():
            here = (pl.ds(r, tile_r), pl.ds(base + c, tile_c))
            clipped = factor * sv[here]
            new_first = 0.9 * mv[here] + 0.1 * clipped
            new_second = 0.95 * vv[here] + 0.05 * clipped * clipped
            master = wv[here]
            new_master = master - 0.01 * (
                (new_first * (1.0 / first_bias))
                / (jnp.sqrt(new_second * (1.0 / second_bias)) + 1e-08)
                + 0.1 * master
            )
            pv[here] = new_master.astype(jnp.bfloat16)
            wv[here] = new_master
            mv[here] = new_first
            vv[here] = new_second

    mine = block(y, x)
    update(0)
    gather_a = [
        send(pv.at[:, cols_a], fa.at[j - 1], {"dp": y * nx + at_x(j)}) for j in range(1, nx)
    ]
    direct = [
        send(pv.at[:, cols_a], out_p.at[mine, cols_a], {"dp": at_y(k) * nx + x})
        for k in range(1, ny)
    ]
    update(half)
    gather_b = [
        send(pv.at[:, cols_b], fb.at[k - 1], {"dp": at_y(k) * nx + x}) for k in range(1, ny)
    ]
    direct += [
        send(pv.at[:, cols_b], out_p.at[mine, cols_b], {"dp": y * nx + at_x(j)})
        for j in range(1, nx)
    ]
    outs = [local(pv, out_p.at[mine]), local(wv, out_w), local(mv, out_m), local(vv, out_v)]
    for j in range(1, nx):
        gather_a[j - 1].wait_recv()
        owner = block(y, lax.rem(x - j + nx, nx))
        for k in range(1, ny):
            direct.append(
                send(fa.at[j - 1], out_p.at[owner, cols_a], {"dp": at_y(k) * nx + x})
            )
        outs.append(local(fa.at[j - 1], out_p.at[owner, cols_a]))
    for k in range(1, ny):
        gather_b[k - 1].wait_recv()
        owner = block(lax.rem(y - k + ny, ny), x)
        for j in range(1, nx):
            direct.append(
                send(fb.at[k - 1], out_p.at[owner, cols_b], {"dp": y * nx + at_x(j)})
            )
        outs.append(local(fb.at[k - 1], out_p.at[owner, cols_b]))
    for copy in outs:
        copy.wait()
    for copy in direct:
        copy.wait_recv()
    for copy in started:
        copy.wait_send()


def solution(mesh):
    n_dp, n_sh = mesh.shape["dp"], mesh.shape["shard"]
    ny, nx = grid_of(n_dp)

    def per_device(gradients, master_weights, first_moment, second_moment):
        rows, width = master_weights.shape
        half = width // 2
        f32, bf16 = jnp.float32, jnp.bfloat16
        state = pltpu.VMEM((rows, width), f32)
        copies = copies_of(ny, nx, n_sh)
        hbm = pl.BlockSpec(memory_space=pltpu.HBM)
        return tuple(pl.pallas_call(
            functools.partial(step_kernel, ny, nx, n_sh, rows * n_dp * n_sh * width),
            out_shape=(
                jax.ShapeDtypeStruct((n_dp * rows, width), bf16),
                jax.ShapeDtypeStruct((rows, width), f32),
                jax.ShapeDtypeStruct((rows, width), f32),
                jax.ShapeDtypeStruct((rows, width), f32),
            ),
            in_specs=[hbm] * 4,
            out_specs=(hbm,) * 4,
            scratch_shapes=[
                pltpu.VMEM((n_dp * rows, width), bf16),
                state, state, state, state,
                pltpu.VMEM((rows, width), bf16),
                pltpu.VMEM((max(ny - 1, 1), nx, rows, half), bf16),
                pltpu.VMEM((max(nx - 1, 1), ny, rows, half), bf16),
                pltpu.VMEM((max(nx - 1, 1), rows, half), bf16),
                pltpu.VMEM((max(ny - 1, 1), rows, half), bf16),
                pltpu.VMEM((max(nx - 1, 1), rows, half), bf16),
                pltpu.VMEM((max(ny - 1, 1), rows, half), bf16),
                pltpu.VMEM((max(nx - 1, 1), rows, half), bf16),
                pltpu.VMEM((max(ny - 1, 1), rows, half), bf16),
                pltpu.VMEM((8, 128), f32),
                pltpu.VMEM((max(n_dp - 1, 1), 8, 128), f32),
                pltpu.VMEM((8, 128), f32),
                pltpu.VMEM((max(n_sh - 1, 1), 8, 128), f32),
                pltpu.SemaphoreType.DMA((8 + ny + nx,)),
                pltpu.SemaphoreType.DMA((copies,)),
                pltpu.SemaphoreType.DMA((copies,)),
            ],
            compiler_params=pltpu.CompilerParams(collective_id=0, has_side_effects=True),
        )(gradients, master_weights, first_moment, second_moment))

    in_specs = (
        P("dp", "shard", None),
        P(("shard", "dp"), None),
        P(("shard", "dp"), None),
        P(("shard", "dp"), None),
    )
    out_specs = (
        P("shard", None),
        P(("shard", "dp"), None),
        P(("shard", "dp"), None),
        P(("shard", "dp"), None),
    )
    return jax.shard_map(
        per_device, mesh=mesh, in_specs=in_specs, out_specs=out_specs, check_vma=False
    )
```

time: 104 us -> 38.2 us (0.37)
  waiting for transfers between devices: 55.2 us -> 0 us
  Pallas kernels: 0 us -> 32.2 us
  blocking collectives: 28.5 us -> 0 us
  between operations: 14.8 us -> 0.65 us
  other arithmetic: 4.65 us -> 0 us
  local copies, waits for them, and re-layouts: 0.89 us -> 5.16 us
    psum x1 -> x0, waiting for transfers between devices: 54.5 us -> none  [per_device(): lax.psum(local_grad.astype(jnp.bfloat16), 'dp').astype(jnp.float32)]
    pallas_call x0 -> x1, Pallas kernels: none -> 32.2 us  [per_device(): pl.pallas_call(functools.partial(step_kernel, ny, nx, n_sh, rows * n_dp *...]
    psum x1 -> x0, blocking collectives: 16.9 us -> none  [per_device(): square_sum = lax.psum(jnp.sum(group_sum * group_sum), 'shard')]
    all_gather x1 -> x0, blocking collectives: 11.7 us -> none  [per_device(): parameters = lax.all_gather(owned_params, 'dp', axis=0, tiled=True)]
    unnamed x7 -> x10, local copies, waits for them, and re-layouts: 0.89 us -> 5.16 us
    convert_element_type x2 -> x0, other arithmetic: 2.51 us -> none  [the longest x1 1.3 us: per_device(): lax.psum(local_grad.astype(jnp.bfloat16), 'dp').astype(jnp.float32)]
    reduce_sum x1 -> x0, other arithmetic: 2.14 us -> none  [per_device(): square_sum = lax.psum(jnp.sum(group_sum * group_sum), 'shard')]
  transfers between devices with their start and end apart: 1 -> 0, of which waited for: 1 -> 0; matrix products, arithmetic and copies ran while one was open for 0% -> 0% of each run, Pallas kernels for 0% -> 0%
where the time goes in v1:
time: 38.2 us; the launch traced here: 38 us
  Pallas kernels  32.2 us (84%)
  local copies, waits for them, and re-layouts  5.16 us (14%)
  between operations  0.65 us (2%)
    pallas_call x1, Pallas kernels, per_device(): pl.pallas_call(functools.partial(step_kernel, ny, nx, n_sh, rows * n_dp *...  32.2 us
    unnamed x10, local copies, waits for them, and re-layouts  5.16 us

profile of v1, /device:TPU:0, one launch (start us, length us, event | category | flops | bytes accessed | tf_op | source)
XLA Modules:
  0.0 38.0 jit_solution(4822035223613275820)
XLA Ops:
  0.6 32.2 %shard_map.75 = (bf16[192,2048]{1,0:T(8,128)(2,1)}, f32[48,2048]{1,0:T(8,128)}, f32[48,2048]{1,0:T(8,128)}, f32[48,2048]{1,0:T(8,128)}) custom-call(bf16[1,192,2048]{2,1,0:T(8,128)(2,1)} %g.1, f32[48,2048]{1,0:T(8,128)} %w.1, f32[48,2048]{1,0:T(8,128)} %m.1, f32[48,2048]{1,0:T(8,128)} %v.1), custom_call_target="tpu_custom_call" | custom-call | tf_op jit(solution)/shard_map/pallas_call | solution.py:248
  32.8 0.0 copy-start.2
  32.8 2.1 %copy.12 = bf16[192,2048]{1,0:T(8,128)(2,1)} copy(bf16[192,2048]{1,0:T(8,128)(2,1)} %get-tuple-element.8) | data formatting | bytes 1572864
  34.9 0.0 copy-done.2
  34.9 0.0 copy-start.1
  34.9 0.7 %copy.13 = f32[48,2048]{1,0:T(8,128)} copy(f32[48,2048]{1,0:T(8,128)S(1)} %copy-done.2) | data formatting | bytes 786432
  35.7 0.4 %copy-done.1 = f32[48,2048]{1,0:T(8,128)S(1)} copy-done((f32[48,2048]{1,0:T(8,128)S(1)}, f32[48,2048]{1,0:T(8,128)}, u32[]{:S(2)}) %copy-start.1) | copy-done | bytes 393240
  36.1 0.0 copy-start
  36.1 0.7 %copy.14 = f32[48,2048]{1,0:T(8,128)} copy(f32[48,2048]{1,0:T(8,128)S(1)} %copy-done.1) | data formatting | bytes 786432
  36.8 0.4 %copy-done = f32[48,2048]{1,0:T(8,128)S(1)} copy-done((f32[48,2048]{1,0:T(8,128)S(1)}, f32[48,2048]{1,0:T(8,128)}, u32[]{:S(2)}) %copy-start) | copy-done | bytes 393240
  37.2 0.7 %copy.15 = f32[48,2048]{1,0:T(8,128)} copy(f32[48,2048]{1,0:T(8,128)S(1)} %copy-done) | data formatting | bytes 786432
Async XLA Ops:
  32.8 2.2 %copy-start.2 = (f32[48,2048]{1,0:T(8,128)S(1)}, f32[48,2048]{1,0:T(8,128)}, u32[]{:S(2)}) copy-start(f32[48,2048]{1,0:T(8,128)} %get-tuple-element.9) | copy-start | bytes 1179652
  34.9 1.1 %copy-start.1 = (f32[48,2048]{1,0:T(8,128)S(1)}, f32[48,2048]{1,0:T(8,128)}, u32[]{:S(2)}) copy-start(f32[48,2048]{1,0:T(8,128)} %get-tuple-element.10) | copy-start | bytes 1179652
  36.1 1.1 %copy-start = (f32[48,2048]{1,0:T(8,128)S(1)}, f32[48,2048]{1,0:T(8,128)}, u32[]{:S(2)}) copy-start(f32[48,2048]{1,0:T(8,128)} %get-tuple-element.11) | copy-start | bytes 1179652

commit v2 on v1

v2 whole, which is shorter than its diff:
```python
import functools
import math

import jax
import jax.numpy as jnp
from jax import lax
from jax.experimental import pallas as pl
from jax.experimental.pallas import tpu as pltpu
from jax.sharding import PartitionSpec as P

MESH = pl.DeviceIdType.MESH
CHUNKS = 2
first_bias = 1.0 - math.exp(100.0 * math.log(0.9))
second_bias = 1.0 - math.exp(100.0 * math.log(0.95))


def grid_of(n_dp):
    ny = max(d for d in range(1, math.isqrt(n_dp) + 1) if n_dp % d == 0)
    return ny, n_dp // ny


def copies_of(ny, nx, n_sh):
    moves = 3 * (ny * nx - 1) * 2 * CHUNKS
    scalars = ny * nx * n_sh if ny * nx * n_sh <= 64 else ny * nx + n_sh
    return moves + scalars


def step_kernel(
    ny, nx, n_sh, entries,
    g, w, m, v,
    out_p, wv, mv, vv,
    gv, sv,
    r1a, r1b, s2a, s2b, r2a, r2b,
    d_own, d_in, h_own, met,
    lsem, ssem, rsem,
):
    n_dp = ny * nx
    rows, width = w.shape
    half = width // 2
    tile_r = 16 if rows % 16 == 0 else rows
    tile_c = min(512, half // CHUNKS)
    me = lax.axis_index("dp")
    sh = lax.axis_index("shard")
    y, x = me // nx, lax.rem(me, nx)
    count = [0]
    local_count = [0]
    started = []

    def at_y(k):
        return lax.rem(y + k, ny)

    def at_x(j):
        return lax.rem(x + j, nx)

    def block(by, bx):
        return pl.ds(pl.multiple_of((by * nx + bx) * rows, rows), rows)

    def send(src, dst, target):
        i = count[0]
        count[0] += 1
        copy = pltpu.make_async_remote_copy(
            src_ref=src, dst_ref=dst, send_sem=ssem.at[i], recv_sem=rsem.at[i],
            device_id=target, device_id_type=MESH,
        )
        copy.start()
        started.append(copy)
        return copy

    def local(src, dst):
        i = local_count[0]
        local_count[0] += 1
        copy = pltpu.make_async_copy(src, dst, lsem.at[i])
        copy.start()
        return copy

    barrier = pltpu.get_barrier_semaphore()
    for i in range(1, n_dp):
        pl.semaphore_signal(
            barrier, inc=1, device_id={"dp": lax.rem(me + i, n_dp)}, device_id_type=MESH
        )
    for i in range(1, n_sh):
        pl.semaphore_signal(
            barrier, inc=1, device_id={"shard": lax.rem(sh + i, n_sh)}, device_id_type=MESH
        )
    gap = half // CHUNKS
    order = [(at_y(k), at_x(j)) for k in range(1, ny) for j in range(1, nx)]
    order += [(at_y(k), x) for k in range(1, ny)] + [(y, at_x(j)) for j in range(1, nx)]
    grads_in = [local(g.at[0, block(*b)], gv.at[block(*b)]) for b in order + [(y, x)]]
    pl.semaphore_wait(barrier, n_dp - 1 + n_sh - 1)
    for i in range(1, n_sh):
        pl.semaphore_signal(
            met, inc=1, device_id={"shard": lax.rem(sh + i, n_sh)}, device_id_type=MESH
        )

    def cols(base, c):
        return pl.ds(base + c * gap, gap)

    def tiles():
        for r in range(0, rows, tile_r):
            for c in range(0, gap, tile_c):
                yield r, c

    def own_rows(by, bx, r):
        start = pl.multiple_of((by * nx + bx) * rows + r, tile_r)
        return pl.ds(start, tile_r)

    def first_sends(relayed):
        for c in range(CHUNKS):
            for j in (range(1, nx) if relayed else (0,)):
                for k in range(1, ny):
                    first_a[k, j, c] = send(
                        gv.at[block(at_y(k), at_x(j)), cols(0, c)],
                        r1a.at[k - 1, j, :, cols(0, c)], {"dp": at_y(k) * nx + x},
                    )
            for k in (range(1, ny) if relayed else (0,)):
                for j in range(1, nx):
                    first_b[j, k, c] = send(
                        gv.at[block(at_y(k), at_x(j)), cols(half, c)],
                        r1b.at[j - 1, k, :, cols(0, c)], {"dp": y * nx + at_x(j)},
                    )

    first_a, first_b = {}, {}
    relayed = (ny - 1) * (nx - 1)
    for copy in grads_in[:relayed]:
        copy.wait()
    first_sends(True)
    for copy in grads_in[relayed:]:
        copy.wait()
    first_sends(False)
    state_in = [local(w, wv), local(m, mv), local(v, vv)]

    second_a, second_b = {}, {}
    for chunk in range(CHUNKS):
        for j in range(1, nx):
            for k in range(1, ny):
                first_a[k, j, chunk].wait_recv()
            for r, c in tiles():
                here = (pl.ds(r, tile_r), pl.ds(chunk * gap + c, tile_c))
                part = gv[(own_rows(y, at_x(j), r),) + here[1:]].astype(jnp.float32)
                for k in range(1, ny):
                    part = part + r1a[(k - 1, j) + here].astype(jnp.float32)
                s2a[(j - 1,) + here] = part.astype(jnp.bfloat16)
            piece = (j - 1, slice(None), cols(0, chunk))
            second_a[j, chunk] = send(s2a.at[piece], r2a.at[piece], {"dp": y * nx + at_x(j)})
        for k in range(1, ny):
            for j in range(1, nx):
                first_b[j, k, chunk].wait_recv()
            for r, c in tiles():
                here = (pl.ds(r, tile_r), pl.ds(chunk * gap + c, tile_c))
                part = gv[
                    own_rows(at_y(k), x, r), pl.ds(half + chunk * gap + c, tile_c)
                ].astype(jnp.float32)
                for j in range(1, nx):
                    part = part + r1b[(j - 1, k) + here].astype(jnp.float32)
                s2b[(k - 1,) + here] = part.astype(jnp.bfloat16)
            piece = (k - 1, slice(None), cols(0, chunk))
            second_b[k, chunk] = send(s2b.at[piece], r2b.at[piece], {"dp": at_y(k) * nx + x})

    squares = jnp.zeros((8, 128), jnp.float32)
    for chunk in range(CHUNKS):
        for base, first, first_n, second, second_n, early, late in (
            (0, r1a, ny, r2a, nx, first_a, second_a), (half, r1b, nx, r2b, ny, first_b, second_b)
        ):
            for i in range(1, first_n):
                early[i, 0, chunk].wait_recv()
            for i in range(1, second_n):
                late[i, chunk].wait_recv()
            for r, c in tiles():
                here = (pl.ds(r, tile_r), pl.ds(chunk * gap + c, tile_c))
                there = pl.ds(base + chunk * gap + c, tile_c)
                total = gv[own_rows(y, x, r), there].astype(jnp.float32)
                for i in range(1, first_n):
                    total = total + first[(i - 1, 0) + here].astype(jnp.float32)
                for i in range(1, second_n):
                    total = total + second[(i - 1,) + here].astype(jnp.float32)
                sv[pl.ds(r, tile_r), there] = total
                square = total * total
                for a in range(0, tile_r, 8):
                    for b in range(0, tile_c, 128):
                        squares = squares + square[a:a + 8, b:b + 128]

    pl.semaphore_wait(met, n_sh - 1)
    squares = jnp.sum(squares, axis=0, keepdims=True)
    d_own[...] = squares
    if n_dp * n_sh <= 64:
        exchanged = [
            send(d_own, d_in.at[s * n_dp + d - 1],
                 {"dp": lax.rem(me + d, n_dp), "shard": lax.rem(sh + s, n_sh)})
            for s in reversed(range(n_sh)) for d in reversed(range(n_dp)) if s or d
        ]
        for copy in state_in:
            copy.wait()
        for copy in reversed(exchanged):
            copy.wait_recv()
        squares = squares + jnp.sum(d_in[...], axis=0)
    else:
        over_dp = [
            send(d_own, d_in.at[i - 1], {"dp": lax.rem(me + i, n_dp)}) for i in range(1, n_dp)
        ]
        for i, copy in enumerate(over_dp):
            copy.wait_recv()
            squares = squares + d_in[i]
        h_own[...] = squares
        over_sh = [
            send(h_own, d_in.at[n_dp + i - 1], {"shard": lax.rem(sh + i, n_sh)})
            for i in range(1, n_sh)
        ]
        for copy in state_in:
            copy.wait()
        for i, copy in enumerate(over_sh):
            copy.wait_recv()
            squares = squares + d_in[n_dp + i]
    square_sum = jnp.sum(squares, axis=1, keepdims=True)
    limit = 0.5 * math.sqrt(entries)
    factor = jnp.minimum(1.0, limit / jnp.sqrt(square_sum + 1e-06))

    def update(base):
        for r, c in tiles():
            here = (pl.ds(r, tile_r), pl.ds(base + c, tile_c))
            clipped = factor * sv[here]
            new_first = 0.9 * mv[here] + 0.1 * clipped
            new_second = 0.95 * vv[here] + 0.05 * clipped * clipped
            master = wv[here]
            new_master = master - 0.01 * (
                (new_first * (1.0 / first_bias))
                / (jnp.sqrt(new_second * (1.0 / second_bias)) + 1e-08)
                + 0.1 * master
            )
            out_p[own_rows(y, x, r), pl.ds(base + c, tile_c)] = new_master.astype(jnp.bfloat16)
            wv[here] = new_master
            mv[here] = new_first
            vv[here] = new_second

    def spread(owner, where, target):
        return send(out_p.at[owner, where], out_p.at[owner, where], target)

    mine = block(y, x)
    gather_a, gather_b, last = {}, {}, []
    for c in range(CHUNKS):
        update(c * gap)
        for j in range(1, nx):
            gather_a[j, c] = spread(mine, cols(0, c), {"dp": y * nx + at_x(j)})
        update(half + c * gap)
        for k in range(1, ny):
            gather_b[k, c] = spread(mine, cols(half, c), {"dp": at_y(k) * nx + x})
    for c in range(CHUNKS):
        last += [spread(mine, cols(0, c), {"dp": at_y(k) * nx + x}) for k in range(1, ny)]
        last += [spread(mine, cols(half, c), {"dp": y * nx + at_x(j)}) for j in range(1, nx)]
    for c in range(CHUNKS):
        for j in range(1, nx):
            gather_a[j, c].wait_recv()
            owner = block(y, lax.rem(x - j + nx, nx))
            last += [spread(owner, cols(0, c), {"dp": at_y(k) * nx + x}) for k in range(1, ny)]
        for k in range(1, ny):
            gather_b[k, c].wait_recv()
            owner = block(lax.rem(y - k + ny, ny), x)
            last += [spread(owner, cols(half, c), {"dp": y * nx + at_x(j)}) for j in range(1, nx)]
    for copy in last:
        copy.wait_recv()
    for copy in started:
        copy.wait_send()


def write_kernel(*refs):
    n = (len(refs) - 1) // 2
    sems = refs[-1]
    copies = [pltpu.make_async_copy(refs[i], refs[n + i], sems.at[i]) for i in range(n)]
    for copy in copies:
        copy.start()
    for copy in copies:
        copy.wait()


def write_out(arrays):
    n = len(arrays)
    size = sum(a.size * a.dtype.itemsize for a in arrays)
    return tuple(pl.pallas_call(
        write_kernel,
        out_shape=tuple(jax.ShapeDtypeStruct(a.shape, a.dtype) for a in arrays),
        in_specs=[pl.BlockSpec(memory_space=pltpu.VMEM)] * n,
        out_specs=(pl.BlockSpec(memory_space=pltpu.HBM),) * n,
        scratch_shapes=[pltpu.SemaphoreType.DMA((n,))],
        compiler_params=pltpu.CompilerParams(vmem_limit_bytes=2 * size + 2**20),
    )(*arrays))


def solution(mesh):
    n_dp, n_sh = mesh.shape["dp"], mesh.shape["shard"]
    ny, nx = grid_of(n_dp)

    def per_device(gradients, master_weights, first_moment, second_moment):
        rows, width = master_weights.shape
        half = width // 2
        f32, bf16 = jnp.float32, jnp.bfloat16
        copies = copies_of(ny, nx, n_sh)
        scalars = n_dp * n_sh - 1 if n_dp * n_sh <= 64 else n_dp + n_sh
        vmem = 24 * (n_dp + 4) * rows * width
        hbm = pl.BlockSpec(memory_space=pltpu.HBM)
        inputs = [
            pltpu.with_memory_space_constraint(a, pltpu.HBM)
            for a in (gradients, master_weights, first_moment, second_moment)
        ]
        return write_out(pl.pallas_call(
            functools.partial(step_kernel, ny, nx, n_sh, rows * n_dp * n_sh * width),
            out_shape=(
                jax.ShapeDtypeStruct((n_dp * rows, width), bf16),
                jax.ShapeDtypeStruct((rows, width), f32),
                jax.ShapeDtypeStruct((rows, width), f32),
                jax.ShapeDtypeStruct((rows, width), f32),
            ),
            in_specs=[hbm] * 4,
            out_specs=(pl.BlockSpec(memory_space=pltpu.VMEM),) * 4,
            scratch_shapes=[
                pltpu.VMEM((n_dp * rows, width), bf16),
                pltpu.VMEM((rows, width), f32),
                pltpu.VMEM((max(ny - 1, 1), nx, rows, half), bf16),
                pltpu.VMEM((max(nx - 1, 1), ny, rows, half), bf16),
                pltpu.VMEM((max(nx - 1, 1), rows, half), bf16),
                pltpu.VMEM((max(ny - 1, 1), rows, half), bf16),
                pltpu.VMEM((max(nx - 1, 1), rows, half), bf16),
                pltpu.VMEM((max(ny - 1, 1), rows, half), bf16),
                pltpu.VMEM((1, 128), f32),
                pltpu.VMEM((scalars, 1, 128), f32),
                pltpu.VMEM((1, 128), f32),
                pltpu.SemaphoreType.REGULAR,
                pltpu.SemaphoreType.DMA((n_dp + 3,)),
                pltpu.SemaphoreType.DMA((copies,)),
                pltpu.SemaphoreType.DMA((copies,)),
            ],
            compiler_params=pltpu.CompilerParams(
                collective_id=0, has_side_effects=True, vmem_limit_bytes=vmem
            ),
        )(*inputs))

    in_specs = (
        P("dp", "shard", None),
        P(("shard", "dp"), None),
        P(("shard", "dp"), None),
        P(("shard", "dp"), None),
    )
    out_specs = (
        P("shard", None),
        P(("shard", "dp"), None),
        P(("shard", "dp"), None),
        P(("shard", "dp"), None),
    )
    return jax.shard_map(
        per_device, mesh=mesh, in_specs=in_specs, out_specs=out_specs, check_vma=False
    )
```

time: 38.2 us -> 29.7 us (0.78)
  local copies, waits for them, and re-layouts: 5.16 us -> 0 us
  Pallas kernels: 32.2 us -> 29 us
    unnamed x10 -> x0, local copies, waits for them, and re-layouts: 5.16 us -> none
    pallas_call x1, Pallas kernels: 32.2 us -> 27.7 us  [per_device(): pl.pallas_call(functools.partial(step_kernel, ny, nx, n_sh, rows * n_dp *...]
    pallas_call x0 -> x1, Pallas kernels: none -> 1.3 us  [write_out(): pl.pallas_call(write_kernel, out_shape=tuple((jax.ShapeDtypeStruct(a.shap...]
where the time goes in v2:
time: 29.7 us; the launch traced here: 29.6 us
  Pallas kernels  29 us (98%)
  between operations  0.64 us (2%)
    pallas_call x1, Pallas kernels, per_device(): pl.pallas_call(functools.partial(step_kernel, ny, nx, n_sh, rows * n_dp *...  27.7 us
    pallas_call x1, Pallas kernels, write_out(): pl.pallas_call(write_kernel, out_shape=tuple((jax.ShapeDtypeStruct(a.shap...  1.3 us

profile of v2, /device:TPU:0, one launch (start us, length us, event | category | flops | bytes accessed | tf_op | source)
XLA Modules:
  0.0 29.6 jit_solution(16930953794032866741)
XLA Ops:
  0.6 27.7 %shard_map.75 = (bf16[192,2048]{1,0:T(8,128)(2,1)S(1)}, f32[48,2048]{1,0:T(8,128)S(1)}, f32[48,2048]{1,0:T(8,128)S(1)}, f32[48,2048]{1,0:T(8,128)S(1)}) custom-call(bf16[1,192,2048]{2,1,0:T(8,128)(2,1)} %g.1, f32[48,2048]{1,0:T(8,128)} %w.1, f32[48,2048]{1,0:T(8,128)} %m.1, f32[48,2048]{1,0:T(8,128)} %v.1), custom_call_target="tpu_custom_call" | custom-call | tf_op jit(solution)/shard_map/pallas_call | solution.py:303
  28.3 1.3 %shard_map.76 = (bf16[192,2048]{1,0:T(8,128)(2,1)}, f32[48,2048]{1,0:T(8,128)}, f32[48,2048]{1,0:T(8,128)}, f32[48,2048]{1,0:T(8,128)}) custom-call(bf16[192,2048]{1,0:T(8,128)(2,1)S(1)} %get-tuple-element.8.refs_0_, f32[48,2048]{1,0:T(8,128)S(1)} %get-tuple-element.9.refs_1_, f32[48,2048]{1,0:T(8,128)S(1)} %get-tuple-element.10.refs_2_, ...), custom_call_target="tpu_custom_call" | custom-call | tf_op jit(solution)/shard_map/pallas_call | solution.py:277

commit v3 on v2

--- a/solution.py
+++ b/solution.py
@@ -179,6 +179,15 @@
                     for b in range(0, tile_c, 128):
                         squares = squares + square[a:a + 8, b:b + 128]
 
+    def decay():
+        for copy in state_in:
+            copy.wait()
+        for base in range(0, width, gap):
+            for r, c in tiles():
+                here = (pl.ds(r, tile_r), pl.ds(base + c, tile_c))
+                mv[here] = 0.9 * mv[here]
+                vv[here] = 0.95 * vv[here]
+
     pl.semaphore_wait(met, n_sh - 1)
     squares = jnp.sum(squares, axis=0, keepdims=True)
     d_own[...] = squares
@@ -188,8 +197,7 @@
                  {"dp": lax.rem(me + d, n_dp), "shard": lax.rem(sh + s, n_sh)})
             for s in reversed(range(n_sh)) for d in reversed(range(n_dp)) if s or d
         ]
-        for copy in state_in:
-            copy.wait()
+        decay()
         for copy in reversed(exchanged):
             copy.wait_recv()
         squares = squares + jnp.sum(d_in[...], axis=0)
@@ -205,8 +213,7 @@
             send(h_own, d_in.at[n_dp + i - 1], {"shard": lax.rem(sh + i, n_sh)})
             for i in range(1, n_sh)
         ]
-        for copy in state_in:
-            copy.wait()
+        decay()
         for i, copy in enumerate(over_sh):
             copy.wait_recv()
             squares = squares + d_in[n_dp + i]
@@ -218,8 +225,8 @@
         for r, c in tiles():
             here = (pl.ds(r, tile_r), pl.ds(base + c, tile_c))
             clipped = factor * sv[here]
-            new_first = 0.9 * mv[here] + 0.1 * clipped
-            new_second = 0.95 * vv[here] + 0.05 * clipped * clipped
+            new_first = mv[here] + 0.1 * clipped
+            new_second = vv[here] + 0.05 * clipped * clipped
             master = wv[here]
             new_master = master - 0.01 * (
                 (new_first * (1.0 / first_bias))

time: 29.7 us -> 29.7 us (level)
  no operation moved by 1% of the time
where the time goes in v3:
time: 29.7 us; the launch traced here: 29.6 us
  Pallas kernels  28.9 us (97%)
  between operations  0.64 us (2%)
    pallas_call x1, Pallas kernels, per_device(): pl.pallas_call(functools.partial(step_kernel, ny, nx, n_sh, rows * n_dp *...  27.6 us
    pallas_call x1, Pallas kernels, write_out(): pl.pallas_call(write_kernel, out_shape=tuple((jax.ShapeDtypeStruct(a.shap...  1.3 us

profile of v3, /device:TPU:0, one launch (start us, length us, event | category | flops | bytes accessed | tf_op | source)
XLA Modules:
  0.0 29.6 jit_solution(13400628794947418821)
XLA Ops:
  0.6 27.6 %shard_map.75 = (bf16[192,2048]{1,0:T(8,128)(2,1)S(1)}, f32[48,2048]{1,0:T(8,128)S(1)}, f32[48,2048]{1,0:T(8,128)S(1)}, f32[48,2048]{1,0:T(8,128)S(1)}) custom-call(bf16[1,192,2048]{2,1,0:T(8,128)(2,1)} %g.1, f32[48,2048]{1,0:T(8,128)} %w.1, f32[48,2048]{1,0:T(8,128)} %m.1, f32[48,2048]{1,0:T(8,128)} %v.1), custom_call_target="tpu_custom_call" | custom-call | tf_op jit(solution)/shard_map/pallas_call | solution.py:310
  28.3 1.3 %shard_map.76 = (bf16[192,2048]{1,0:T(8,128)(2,1)}, f32[48,2048]{1,0:T(8,128)}, f32[48,2048]{1,0:T(8,128)}, f32[48,2048]{1,0:T(8,128)}) custom-call(bf16[192,2048]{1,0:T(8,128)(2,1)S(1)} %get-tuple-element.8.refs_0_, f32[48,2048]{1,0:T(8,128)S(1)} %get-tuple-element.9.refs_1_, f32[48,2048]{1,0:T(8,128)S(1)} %get-tuple-element.10.refs_2_, ...), custom_call_target="tpu_custom_call" | custom-call | tf_op jit(solution)/shard_map/pallas_call | solution.py:284
